TPU v7x, 32 devices: a whole 2x2x4 slice. The times are simulated.
32 devices in a mesh: sub: 8 (over z, x), grp: 4 (over y, core).
Axes of the slice: x: 2, y: 2, z: 4, core: 2. Of those that a mesh axis runs over, the one named last changes fastest.
Arguments:
- solution: float32 [32, 128, 2048], P(('sub', 'grp')), may hold values from -6 to 6
- residual: float32 [32, 128, 2048], P(('sub', 'grp'))
- direction: float32 [32, 128, 2048], P(('sub', 'grp'))
- residual_product: float32 [128], replicated, may hold values from 65536 to 1310720
- neighbor_slots: int32 [32, 4], P(('sub', 'grp')), may hold values from 0 to 3, each once within a row
- coupling: bfloat16 [32, 96, 256, 128], P(('sub', 'grp')), may hold values from -0.375 to 0.375
- dirichlet_factor: bfloat16 [32, 96, 128, 128], P(('sub', 'grp')), may hold values from -0.5 to 0.5
- face_block: bfloat16 [32, 32, 128, 128], P(('sub', 'grp')), as said below
- neumann_factor: bfloat16 [32, 32, 128, 128], P(('sub', 'grp')), may hold values from -0.5 to 0.5
- primal_block: int32 [32, 128], P(('sub', 'grp')), may hold values from 0 to 31
- primal_basis: bfloat16 [32, 128, 128], P(('sub', 'grp')), may hold values from -1.5 to 1.5
- coarse_matrix: float32 [32, 9, 128, 128], P(('sub', 'grp')), may hold values from -0.17677669 to 0.17677669
- coarse_block_inverse: float32 [32, 128, 128], P(('sub', 'grp')), may hold values from -0.5 to 0.5
- coarse_pattern: int32 [32, 9], P(('sub', 'grp')), may hold values from 0 to 31, as said below
Outputs:
- new_solution: float32 [32, 128, 2048], P(('sub', 'grp'))
- new_residual: float32 [32, 128, 2048], P(('sub', 'grp'))
- new_direction: float32 [32, 128, 2048], P(('sub', 'grp'))
- new_product: float32 [128], replicated
Inputs may be any that keep to these rules, and one draw needn't show every extreme that they name: `neighbor_slots`: each row orders the four local face slots: entry d is the slot of the face toward direction d (sub lower, sub upper, grp lower, grp upper). `coarse_pattern`: row t names 9 different subdomains, the first of them t itself; subdomain s lies on the device of index s along sub+grp, and every entry lies within 2 positions of row t along sub, cyclically. `face_block`: each block is symmetric with every eigenvalue at least 0.5.
All inputs are finite; a program needn't handle non-finite values.
Results may differ from a plain program's by a relative error of at most 0.0003.
Values sent between devices are 32-bit elements; how exact they have to be, the bound alone decides.
A program may use at most 128 MiB of HBM per device.

v0:
```python
import jax
import jax.numpy as jnp
from jax import lax
from jax.sharding import PartitionSpec as P

REACH_SUBS = 2


highest_precision = lax.Precision.HIGHEST


def shifted(value, axis, steps):
    count = lax.axis_size(axis)
    pairs = [(source, (source + steps) % count) for source in range(count)]
    return lax.ppermute(value, axis, pairs)


def slot_table(neighbor_slots):
    return (neighbor_slots[0][:, None] == jnp.arange(4, dtype=jnp.int32)[None, :]).astype(
        jnp.float32
    )


def place_faces(directed, slot_onehot, block_width):
    load_count = directed.shape[1]
    face_width = directed.shape[2]
    placed = jnp.einsum("dk,dlf->lkf", slot_onehot, directed, precision=highest_precision)
    return placed.reshape(load_count, 4 * face_width // block_width, block_width)


def spread(owned_part, slot_onehot, block_width):
    face_width = owned_part.shape[2] // 2
    own_sub = owned_part[:, :, :face_width]
    own_grp = owned_part[:, :, face_width:]
    from_sub = shifted(own_sub, "sub", 1)
    from_grp = shifted(own_grp, "grp", 1)
    directed = jnp.stack([from_sub[0], own_sub[0], from_grp[0], own_grp[0]], 0)
    return place_faces(directed, slot_onehot, block_width)


def collect(local_part, slot_onehot):
    load_count = local_part.shape[0]
    placed = local_part.reshape(load_count, 4, -1)
    directed = jnp.einsum("dk,lkf->dlf", slot_onehot, placed, precision=highest_precision)
    to_sub = shifted(directed[0][None], "sub", -1)
    to_grp = shifted(directed[2][None], "grp", -1)
    owned_sub = directed[1][None] + to_sub
    owned_grp = directed[3][None] + to_grp
    return jnp.concatenate([owned_sub, owned_grp], 2)


def condensed(vector, couple, dirichlet, face_matrix):
    count_of_blocks = vector.shape[1]
    block_width = vector.shape[2]
    paired = jnp.concatenate(
        [
            jnp.concatenate([vector, jnp.roll(vector, -(offset + 1), axis=1)], 2)
            for offset in range(3)
        ],
        1,
    )
    interior = jnp.einsum("lib,ibk->lik", paired, couple, precision=highest_precision)
    middle = jnp.einsum("lik,ikm->lim", interior, dirichlet, precision=highest_precision)
    solved = jnp.einsum("lim,ikm->lik", middle, dirichlet, precision=highest_precision)
    returned = jnp.einsum("lik,ibk->lib", solved, couple, precision=highest_precision)
    result = jnp.einsum("ljb,jbk->ljk", vector, face_matrix, precision=highest_precision)
    for offset in range(3):
        portion = returned[:, offset * count_of_blocks : (offset + 1) * count_of_blocks]
        result = (
            result
            + portion[:, :, :block_width]
            + jnp.roll(portion[:, :, block_width:], offset + 1, axis=1)
        )
    return result


def coarse_neighbors(initial_step, pattern, matrix):
    load_count, primal_count = initial_step.shape
    grp_count = lax.axis_size("grp")
    sub_count = lax.axis_size("sub")
    reach_count = 2 * REACH_SUBS + 1
    entry_sub = pattern // grp_count
    entry_grp = pattern % grp_count
    position = (entry_sub - lax.axis_index("sub") + REACH_SUBS) % sub_count
    column = lax.all_gather(initial_step[None], "grp", axis=0, tiled=True)
    pieces = []
    for place in range(reach_count):
        if place == REACH_SUBS:
            pieces.append(column)
        else:
            pieces.append(shifted(column, "sub", REACH_SUBS - place))
    window = jnp.stack(pieces, 0).reshape(-1, load_count, primal_count)
    slot_index = position * grp_count + entry_grp
    chooser = (slot_index[:, None] == jnp.arange(window.shape[0], dtype=jnp.int32)[None, :]).astype(
        jnp.float32
    )
    chosen = jnp.einsum("kj,jlc->klc", chooser, window, precision=highest_precision)
    return jnp.einsum("klc,kcd->ld", chosen, matrix, precision=highest_precision)


def precondition(
    local_copy, slot_onehot, neumann, block_ids, primal_rows, matrix, inverse, pattern
):
    halved = local_copy * 0.5
    neumann_step = jnp.einsum("ljb,jbk->ljk", halved, neumann, precision=highest_precision)
    local_solve = jnp.einsum("ljk,jmk->ljm", neumann_step, neumann, precision=highest_precision)
    selector = (block_ids[:, None] == jnp.arange(halved.shape[1], dtype=jnp.int32)[None, :]).astype(
        jnp.float32
    )
    picked = jnp.einsum("ljb,cj->lcb", halved, selector, precision=highest_precision)
    coarse_residual = jnp.einsum("lcb,cb->lc", picked, primal_rows, precision=highest_precision)
    initial_step = jnp.dot(coarse_residual, inverse, precision=highest_precision)
    adjacent_sum = coarse_neighbors(initial_step, pattern, matrix)
    coarse_correction = initial_step + jnp.dot(
        coarse_residual - adjacent_sum, inverse, precision=highest_precision
    )
    weighted = coarse_correction[:, :, None] * primal_rows[None]
    spread_back = jnp.einsum("lcb,cj->ljb", weighted, selector, precision=highest_precision)
    return collect(0.5 * (local_solve + spread_back), slot_onehot)


def shards(
    solution,
    residual,
    direction,
    residual_product,
    neighbor_slots,
    coupling,
    dirichlet_factor,
    face_block,
    neumann_factor,
    primal_block,
    primal_basis,
    coarse_matrix,
    coarse_block_inverse,
    coarse_pattern,
):
    slot_onehot = slot_table(neighbor_slots)
    block_width = face_block.shape[2]
    couple = coupling[0].astype(jnp.float32)
    dirichlet = dirichlet_factor[0].astype(jnp.float32)
    face_matrix = face_block[0].astype(jnp.float32)
    neumann = neumann_factor[0].astype(jnp.float32)
    primal_rows = primal_basis[0].astype(jnp.float32)
    direction_local = spread(direction, slot_onehot, block_width)
    image = collect(condensed(direction_local, couple, dirichlet, face_matrix), slot_onehot)
    curvature = lax.psum(jnp.sum(direction * image, axis=(0, 2)), ("sub", "grp"))
    step_length = residual_product / curvature
    new_residual = residual - step_length[None, :, None] * image
    new_local = spread(new_residual, slot_onehot, block_width)
    preconditioned = precondition(
        new_local,
        slot_onehot,
        neumann,
        primal_block[0],
        primal_rows,
        coarse_matrix[0],
        coarse_block_inverse[0],
        coarse_pattern[0],
    )
    new_product = lax.psum(jnp.sum(new_residual * preconditioned, axis=(0, 2)), ("sub", "grp"))
    new_solution = solution + step_length[None, :, None] * direction
    step_ratio = new_product / residual_product
    new_direction = preconditioned + step_ratio[None, :, None] * direction
    return (new_solution, new_residual, new_direction, new_product)


def solution(mesh):
    in_specs = (
        P(("sub", "grp"), None, None),
        P(("sub", "grp"), None, None),
        P(("sub", "grp"), None, None),
        P(),
        P(("sub", "grp"), None),
        P(("sub", "grp"), None, None, None),
        P(("sub", "grp"), None, None, None),
        P(("sub", "grp"), None, None, None),
        P(("sub", "grp"), None, None, None),
        P(("sub", "grp"), None),
        P(("sub", "grp"), None, None),
        P(("sub", "grp"), None, None, None),
        P(("sub", "grp"), None, None),
        P(("sub", "grp"), None),
    )
    out_specs = (
        P(("sub", "grp"), None, None),
        P(("sub", "grp"), None, None),
        P(("sub", "grp"), None, None),
        P(),
    )
    return jax.shard_map(shards, mesh=mesh, in_specs=in_specs, out_specs=out_specs, check_vma=False)
```

profile of v0, /device:TPU:0, one launch (start us, length us, event | category | flops | bytes accessed | tf_op | source)
XLA Modules:
  0.0 302.9 jit_solution(3611158063502701570)
XLA Ops:
  0.7 1.4 fusion.87
  2.1 0.5 copy.70
  2.6 3.0 collective-permute-start
  5.7 0.5 copy.71
  6.3 14.4 %collective-permute-done = f32[1,128,1024]{2,0,1:T(1,128)S(1)} collective-permute-done((f32[1,128,1024]{2,0,1:T(1,128)S(1)}, f32[1,128,1024]{2,0,1:T(1,128)S(1)}, u32[]{:S(2)}, u32[]{:S(2)}) %collective-permute-start) | collective-permute-done | bytes 524320 | tf_op jit(solution)/shard_map/ppermute | solution.py:15
  20.6 5.2 %fusion.45 = f32[128,4,1024]{2,1,0:T(4,128)} fusion(f32[1,128,1024]{2,0,1:T(1,128)S(1)} %copy.71, f32[1,128,1024]{2,0,1:T(1,128)S(1)} %collective-permute-done.1, f32[1,128,1024]{2,0,1:T(1,128)S(1)} %copy.70, f32[1,128,1024]{2,0,1:T(1,128)S(1)} %collective-permute-done, s32[4]{0:T(128)S(1)} %bitcast.127), kind=kOutput, calls=%fused_computation.46 | convolution fusion | flops 26738704 | bytes 4194320 | tf_op jit(solution)/shard_map/dk,dlf->lkf/dot_general | solution.py:27
  25.8 3.0 %reshape.139 = f32[128,32,128]{2,1,0:T(8,128)} reshape(f32[128,4,1024]{2,1,0:T(4,128)} %fusion.45) | data formatting | bytes 4194304 | tf_op jit(solution)/shard_map/reshape | solution.py:28
  28.8 2.0 slice.138
  30.9 0.2 copy-done.2
  31.1 0.3 slice.140
  31.3 0.3 slice.142
  31.9 6.1 %maximum_maximum_fusion = f32[128,96,256]{2,1,0:T(8,128)} fusion(f32[128,3,128]{2,1,0:T(4,128)S(1)} %slice.143, f32[128,29,128]{2,1,0:T(8,128)S(1)} %slice.142, f32[128,32,128]{2,1,0:T(8,128)S(1)} %copy-done.2, f32[128,2,128]{2,1,0:T(2,128)S(1)} %slice.141, f32[128,30,128]{2,1,0:T(8,128)S(1)} %slice.140, f32[128,1,128]{2,1,0:T(1,128)S(1)} %slice.139, ...), kind=kLoop, calls=%fused_computation | loop fusion | flops 25165824 | bytes 20971520 | tf_op jit(solution)/shard_map/concatenate | solution.py:55
  38.0 21.7 %fusion = f32[96,128,128]{2,1,0:T(8,128)} fusion(f32[128,96,256]{2,1,0:T(8,128)} %maximum_maximum_fusion, bf16[1,96,256,128]{3,2,1,0:T(8,128)(2,1)} %param.19), kind=kOutput, calls=%fused_computation.1 | convolution fusion | flops 4831838208 | bytes 25165824 | tf_op jit(solution)/shard_map/lib,ibk->lik/dot_general | solution.py:62
  59.7 5.3 %fusion.11 = f32[96,128,128]{2,1,0:T(8,128)S(1)} fusion(f32[96,128,128]{2,1,0:T(8,128)} %fusion, bf16[1,96,128,128]{3,2,1,0:T(8,128)(2,1)S(1)} %copy-done), kind=kOutput, calls=%fused_computation.12 | convolution fusion | flops 2415919104 | bytes 15728640 | tf_op jit(solution)/shard_map/lik,ikm->lim/dot_general | solution.py:63
  65.0 8.5 %fusion.9 = f32[96,128,128]{2,1,0:T(8,128)} fusion(f32[96,128,128]{2,1,0:T(8,128)S(1)} %fusion.11, bf16[1,96,128,128]{3,2,1,0:T(8,128)(2,1)S(1)} %copy-done), kind=kOutput, calls=%fused_computation.10 | convolution fusion | flops 2415919104 | bytes 15728640 | tf_op jit(solution)/shard_map/lim,ikm->lik/dot_general | solution.py:64
  73.5 8.4 %fusion.15 = f32[128,96,256]{0,2,1:T(8,128)S(1)} fusion(bf16[1,96,256,128]{3,2,1,0:T(8,128)(2,1)} %param.19, f32[96,128,128]{2,1,0:T(8,128)} %fusion.9), kind=kOutput, calls=%fused_computation.16 | convolution fusion | flops 4831838208 | bytes 25165824 | tf_op jit(solution)/shard_map/lik,ibk->lib/dot_general | solution.py:65
  81.8 0.2 slice.146
  82.0 0.2 slice.149
  82.3 0.2 slice.152
  82.5 1.3 copy-done.3
  83.8 0.3 copy-done.12
  84.1 5.4 %fusion.24 = f32[128,32,128]{0,2,1:T(8,128)} fusion(f32[128,96,256]{0,2,1:T(8,128)S(1)} %fusion.15, f32[128,31,128]{0,2,1:T(8,128)S(1)} %slice.146, f32[128,1,128]{0,2,1:T(8,128)S(1)} %slice.145, f32[128,30,128]{0,2,1:T(8,128)S(1)} %slice.149, f32[128,2,128]{0,2,1:T(8,128)S(1)} %slice.148, f32[128,29,128]{0,2,1:T(8,128)S(1)} %slice.152, ...), kind=kOutput, calls=%fused_computation.22 | convolution fusion | flops 810024960 | bytes 17825792 | tf_op jit(solution)/shard_map/ljb,jbk->ljk/dot_general | solution.py:66
  89.5 3.3 %copy.44 = f32[128,4,1024]{2,1,0:T(4,128)} copy(f32[128,4,1024]{0,2,1:T(8,128)} %bitcast.117) | data formatting | bytes 4194304 | tf_op jit(solution)/shard_map/reshape | solution.py:43
  92.8 3.7 %fusion.82 = f32[4,128,1024]{2,0,1:T(4,128)S(1)} fusion(f32[128,4,1024]{2,1,0:T(4,128)} %copy.44, s32[4]{0:T(128)S(1)} %bitcast.128), kind=kOutput, calls=%fused_computation.102 | convolution fusion | flops 25165840 | bytes 4194320 | tf_op jit(solution)/shard_map/dk,lkf->dlf/dot_general | solution.py:44
  96.5 1.5 fusion.85
  98.1 1.8 collective-permute-start.2
  100.1 11.2 %collective-permute-done.2 = f32[1,128,1024]{2,1,0:T(8,128)S(1)} collective-permute-done((f32[1,128,1024]{2,1,0:T(8,128)S(1)}, f32[1,128,1024]{2,1,0:T(8,128)S(1)}, u32[]{:S(2)}, u32[]{:S(2)}) %collective-permute-start.2) | collective-permute-done | bytes 524320 | tf_op jit(solution)/shard_map/ppermute | solution.py:15
  111.7 39.5 %psum.14 = f32[128]{0:T(128)S(1)} all-reduce(f32[128]{0:T(128)S(1)} %multiply_reduce_fusion.1), channel_id=1, replica_groups=mesh['sub'=8,'grp'=4] {'sub','grp'}, use_global_device_ids=true, to_apply=%region_1.2 | all-reduce | flops 128 | bytes 1024 | tf_op jit(solution)/shard_map/psum | solution.py:147
  151.3 1.4 multiply_subtract_fusion
  152.9 2.3 collective-permute-start.4
  155.2 13.2 %collective-permute-done.4 = f32[1,128,1024]{2,1,0:T(8,128)S(1)} collective-permute-done((f32[1,128,1024]{2,1,0:T(8,128)S(1)}, f32[1,128,1024]{2,1,0:T(8,128)S(1)}, u32[]{:S(2)}, u32[]{:S(2)}) %collective-permute-start.4) | collective-permute-done | bytes 524320 | tf_op jit(solution)/shard_map/ppermute | solution.py:15
  168.5 0.8 copy-done.14
  169.3 1.8 pad_maximum_fusion
  171.1 4.8 %multiply_bitcast_fusion = f32[128,4,1024]{2,1,0:T(4,128)} fusion(f32[4,128,1024]{2,1,0:T(8,128)S(1)} %pad_maximum_fusion, s32[4]{0:T(128)S(1)} %bitcast.129), kind=kOutput, calls=%fused_computation.45 | convolution fusion | flops 25690128 | bytes 4194320 | tf_op jit(solution)/shard_map/dk,dlf->lkf/dot_general | solution.py:27
  175.8 2.5 mul.80
  178.3 3.5 %fusion.66 = f32[128,128,128]{2,0,1:T(8,128)S(1)} fusion(f32[128,32,128]{2,1,0:T(8,128)S(1)} %mul.80, s32[128]{0:T(128)S(1)} %bitcast.131), kind=kOutput, calls=%fused_computation.79 | convolution fusion | flops 805310464 | bytes 10486272 | tf_op jit(solution)/shard_map/ljb,cj->lcb/dot_general | solution.py:110
  181.9 11.0 %fusion.2 = f32[128,1,128]{2,1,0:T(1,128)S(1)} fusion(f32[128,128,128]{2,0,1:T(8,128)S(1)} %fusion.66, bf16[128,128,1]{1,0,2:T(8,128)(2,1)S(1)} %bitcast.126), kind=kOutput, calls=%fused_computation.3 | convolution fusion | flops 25165824 | bytes 8486912 | tf_op jit(solution)/shard_map/lcb,cb->lc/dot_general | solution.py:111
  192.8 0.3 fusion.61
  193.1 5.8 %all-gather = f32[512,128]{1,0:T(8,128)S(1)} all-gather(f32[128,128]{1,0:T(8,128)S(1)} %fusion.61), channel_id=2, replica_groups=mesh['sub'=8,'grp'=4] {'grp'}, dimensions={0}, use_global_device_ids=true | all-gather | bytes 327680 | tf_op jit(solution)/shard_map/all_gather | solution.py:85
  198.9 0.3 collective-permute-start.6
  199.2 0.4 collective-permute-start.7
  199.7 4.3 %collective-permute-start.8 = (f32[4,128,128]{2,1,0:T(8,128)S(1)}, f32[4,128,128]{2,1,0:T(8,128)S(1)}, u32[]{:S(2)}, u32[]{:S(2)}) collective-permute-start(f32[4,128,128]{2,1,0:T(8,128)S(1)} %bitcast.121), channel_id=1, source_target_pairs={{0,28},{4,0},{8,4},{12,8},{16,12},{20,16},{24,20},{28,24},{1,29},{... | collective-permute-start | bytes 786440 | tf_op jit(solution)/shard_map/ppermute | solution.py:15
  204.0 1.7 collective-permute-start.9
  205.7 3.6 %fusion.37 = f32[32,128,128]{2,1,0:T(8,128)} fusion(f32[128,32,128]{2,1,0:T(8,128)S(1)} %mul.80, bf16[1,32,128,128]{3,2,1,0:T(8,128)(2,1)S(1)} %copy-done.9), kind=kOutput, calls=%fused_computation.38 | convolution fusion | flops 805306368 | bytes 5242880 | tf_op jit(solution)/shard_map/ljb,jbk->ljk/dot_general | solution.py:105
  209.3 0.7 collective-permute-done.6
  210.0 3.6 %collective-permute-done.7 = f32[4,128,128]{2,1,0:T(8,128)S(1)} collective-permute-done((f32[4,128,128]{2,1,0:T(8,128)S(1)}, f32[4,128,128]{2,1,0:T(8,128)S(1)}, u32[]{:S(2)}, u32[]{:S(2)}) %collective-permute-start.7) | collective-permute-done | bytes 262176 | tf_op jit(solution)/shard_map/ppermute | solution.py:15
  213.7 0.3 collective-permute-done.8
  214.0 6.6 %collective-permute-done.9 = f32[4,128,128]{2,1,0:T(8,128)S(1)} collective-permute-done((f32[4,128,128]{2,1,0:T(8,128)S(1)}, f32[4,128,128]{2,1,0:T(8,128)S(1)}, u32[]{:S(2)}, u32[]{:S(2)}) %collective-permute-start.9) | collective-permute-done | bytes 262176 | tf_op jit(solution)/shard_map/ppermute | solution.py:15
  220.6 1.4 fusion.50
  222.1 1.2 fusion.54
  223.2 0.3 convolution_add_fusion
  223.5 5.3 %fusion.5 = f32[32,128,128]{2,0,1:T(8,128)} fusion(f32[128,128]{1,0:T(8,128)S(1)} %bitcast_convert_fusion, f32[128,128]{1,0:T(8,128)S(1)} %convolution_add_fusion, s32[128]{0:T(128)S(1)} %bitcast.132), kind=kOutput, calls=%fused_computation.6 | convolution fusion | flops 807407616 | bytes 2228736 | tf_op jit(solution)/shard_map/lcb,cj->ljb/dot_general | solution.py:118
  228.9 3.1 %copy.51 = f32[32,128,128]{1,2,0:T(8,128)} copy(f32[32,128,128]{2,0,1:T(8,128)} %fusion.5) | data formatting | bytes 4194304 | tf_op jit(solution)/shard_map/lcb,cj->ljb/dot_general | solution.py:118
  232.0 5.5 %add_multiply_fusion = f32[32,128,128]{1,2,0:T(8,128)} fusion(f32[32,128,128]{1,2,0:T(8,128)} %copy.51, f32[32,128,128]{2,1,0:T(8,128)S(1)} %copy-done.6, bf16[1,32,128,128]{3,2,1,0:T(8,128)(2,1)} %param.22), kind=kOutput, calls=%fused_computation.44 | convolution fusion | flops 806354944 | bytes 7340032 | tf_op jit(solution)/shard_map/ljk,jmk->ljm/dot_general | solution.py:106
  237.5 3.1 %copy.52 = f32[128,4,1024]{2,1,0:T(4,128)} copy(f32[128,4,1024]{0,2,1:T(8,128)} %bitcast.116) | data formatting | bytes 4194304 | tf_op jit(solution)/shard_map/reshape | solution.py:43
  240.6 3.7 %fusion.80 = f32[4,128,1024]{2,0,1:T(4,128)S(1)} fusion(f32[128,4,1024]{2,1,0:T(4,128)} %copy.52, s32[4]{0:T(128)S(1)} %bitcast.130), kind=kOutput, calls=%fused_computation.101 | convolution fusion | flops 25165840 | bytes 4194320 | tf_op jit(solution)/shard_map/dk,lkf->dlf/dot_general | solution.py:44
  244.3 1.5 fusion.84
  245.9 0.2 collective-permute-start.10
  246.2 0.8 collective-permute-start.11
  247.0 12.8 %collective-permute-done.10 = f32[1,128,1024]{2,1,0:T(8,128)S(1)} collective-permute-done((f32[1,128,1024]{2,1,0:T(8,128)S(1)}, f32[1,128,1024]{2,1,0:T(8,128)S(1)}, u32[]{:S(2)}, u32[]{:S(2)}) %collective-permute-start.10) | collective-permute-done | bytes 524320 | tf_op jit(solution)/shard_map/ppermute | solution.py:15
  260.3 0.4 copy-done.7
  260.8 0.2 copy-done.8
  261.0 38.0 %psum.15 = f32[128]{0:T(128)S(1)} all-reduce(f32[128]{0:T(128)S(1)} %multiply_reduce_fusion), channel_id=1, replica_groups=mesh['sub'=8,'grp'=4] {'sub','grp'}, use_global_device_ids=true, to_apply=%region_3.4 | all-reduce | flops 128 | bytes 1024 | tf_op jit(solution)/shard_map/psum | solution.py:161
  299.0 3.6 %multiply_add_fusion = (f32[1,128,2048]{2,1,0:T(8,128)}, f32[1,128,2048]{2,1,0:T(8,128)}) fusion(f32[1,128,2048]{2,1,0:T(8,128)} %param.16, f32[1,128,1024]{2,1,0:T(8,128)} %copy-done.8, f32[1,128,1024]{2,1,0:T(8,128)} %copy-done.7, f32[128]{0:T(128)S(1)} %div.23, f32[1,128,2048]{2,1,0:T(8,128)} %param.14, f32[128]{0:T(128)S(1)} %div.18), kind=kLoop, calls=%fused_computation.57 | loop fusion | flops 1310720 | bytes 5243904 | tf_op jit(solution)/shard_map/add | solution.py:164
  (71 shorter events, 2.0 us)
Async XLA Ops:
  0.6 59.0 %copy-start = (bf16[1,96,128,128]{3,2,1,0:T(8,128)(2,1)S(1)}, bf16[1,96,128,128]{3,2,1,0:T(8,128)(2,1)}, u32[]{:S(2)}) copy-start(bf16[1,96,128,128]{3,2,1,0:T(8,128)(2,1)} %param.20) | copy-start | bytes 9437188
  0.6 20.0 %copy-start.17 = (s32[1,4]{1,0:T(1,128)S(1)}, s32[1,4]{1,0:T(1,128)}, u32[]{:S(2)}) copy-start(s32[1,4]{1,0:T(1,128)} %param.18) | copy-start | bytes 52
  2.6 18.0 %collective-permute-start = (f32[1,128,1024]{2,0,1:T(1,128)S(1)}, f32[1,128,1024]{2,0,1:T(1,128)S(1)}, u32[]{:S(2)}, u32[]{:S(2)}) collective-permute-start(f32[1,128,1024]{2,0,1:T(1,128)S(1)} %copy.70), channel_id=1, source_target_pairs={{0,4},{4,8},{8,12},{12,16},{16,20},{20,24},{24,28},{28,0},{1,5},{5... | collective-permute-start | bytes 1572872 | tf_op jit(solution)/shard_map/ppermute | solution.py:15
  6.2 14.4 %collective-permute-start.1 = (f32[1,128,1024]{2,0,1:T(1,128)S(1)}, f32[1,128,1024]{2,0,1:T(1,128)S(1)}, u32[]{:S(2)}, u32[]{:S(2)}) collective-permute-start(f32[1,128,1024]{2,0,1:T(1,128)S(1)} %copy.71), channel_id=1, source_target_pairs={{0,1},{1,2},{2,3},{3,0},{4,5},{5,6},{6,7},{7,4},{8,9},{9,10},{10,1... | collective-permute-start | bytes 1572872 | tf_op jit(solution)/shard_map/ppermute | solution.py:15
  28.8 2.2 copy-start.2
  82.2 1.6 copy-start.3
  82.2 1.9 copy-start.12
  98.1 13.1 %collective-permute-start.2 = (f32[1,128,1024]{2,1,0:T(8,128)S(1)}, f32[1,128,1024]{2,1,0:T(8,128)S(1)}, u32[]{:S(2)}, u32[]{:S(2)}) collective-permute-start(f32[1,128,1024]{2,1,0:T(8,128)S(1)} %copy.73), channel_id=1, source_target_pairs={{0,28},{4,0},{8,4},{12,8},{16,12},{20,16},{24,20},{28,24},{1,29},{... | collective-permute-start | bytes 1572872 | tf_op jit(solution)/shard_map/ppermute | solution.py:15
  99.9 11.6 %copy-start.5 = (f32[1,128,2048]{2,1,0:T(8,128)S(1)}, f32[1,128,2048]{2,1,0:T(8,128)}, u32[]{:S(2)}) copy-start(f32[1,128,2048]{2,1,0:T(8,128)} %param.16) | copy-start | bytes 3145732
  100.0 11.4 %collective-permute-start.3 = (f32[1,128,1024]{2,1,0:T(8,128)S(1)}, f32[1,128,1024]{2,1,0:T(8,128)S(1)}, u32[]{:S(2)}, u32[]{:S(2)}) collective-permute-start(f32[1,128,1024]{2,1,0:T(8,128)S(1)} %copy.75), channel_id=1, source_target_pairs={{0,3},{1,0},{2,1},{3,2},{4,7},{5,4},{6,5},{7,6},{8,11},{9,8},{10,9... | collective-permute-start | bytes 1572872 | tf_op jit(solution)/shard_map/ppermute | solution.py:15
  111.4 39.9 %copy-start.20 = (f32[128]{0:T(128)S(1)}, f32[128]{0:T(128)}, u32[]{:S(2)}) copy-start(f32[128]{0:T(128)} %param.17) | copy-start | bytes 1540
  151.3 3.9 %copy-start.19 = (s32[1,9]{1,0:T(1,128)S(1)}, s32[1,9]{1,0:T(1,128)}, u32[]{:S(2)}) copy-start(s32[1,9]{1,0:T(1,128)} %param.27) | copy-start | bytes 112
  151.3 3.9 %copy-start.15 = (bf16[1,128,128]{2,1,0:T(8,128)(2,1)S(1)}, bf16[1,128,128]{2,1,0:T(8,128)(2,1)}, u32[]{:S(2)}) copy-start(bf16[1,128,128]{2,1,0:T(8,128)(2,1)} %param.24) | copy-start | bytes 98308
  152.7 107.4 %copy-start.4 = (f32[1,128,2048]{2,1,0:T(8,128)}, f32[1,128,2048]{2,1,0:T(8,128)S(1)}, u32[]{:S(2)}) copy-start(f32[1,128,2048]{2,1,0:T(8,128)S(1)} %multiply_subtract_fusion) | copy-start | bytes 3145732
  152.8 15.6 %copy-start.10 = (f32[1,128,1024]{2,1,0:T(8,128)}, f32[1,128,1024]{2,1,0:T(8,128)S(1)}, u32[]{:S(2)}) copy-start(f32[1,128,1024]{2,1,0:T(8,128)S(1)} %get-tuple-element.18) | copy-start | bytes 1572868
  152.9 15.6 %copy-start.11 = (f32[1,128,1024]{2,1,0:T(8,128)}, f32[1,128,1024]{2,1,0:T(8,128)S(1)}, u32[]{:S(2)}) copy-start(f32[1,128,1024]{2,1,0:T(8,128)S(1)} %get-tuple-element.19) | copy-start | bytes 1572868
  152.9 15.6 %collective-permute-start.4 = (f32[1,128,1024]{2,1,0:T(8,128)S(1)}, f32[1,128,1024]{2,1,0:T(8,128)S(1)}, u32[]{:S(2)}, u32[]{:S(2)}) collective-permute-start(f32[1,128,1024]{2,1,0:T(8,128)S(1)} %get-tuple-element.18), channel_id=1, source_target_pairs={{0,4},{4,8},{8,12},{12,16},{16,20},{20,24},{24,28},{28,0},{1,5},{5... | collective-permute-start | bytes 1572872 | tf_op jit(solution)/shard_map/ppermute | solution.py:15
  155.2 14.1 %collective-permute-start.5 = (f32[1,128,1024]{2,1,0:T(8,128)S(1)}, f32[1,128,1024]{2,1,0:T(8,128)}, u32[]{:S(2)}, u32[]{:S(2)}) collective-permute-start(f32[1,128,1024]{2,1,0:T(8,128)S(1)} %get-tuple-element.19), channel_id=1, source_target_pairs={{0,1},{1,2},{2,3},{3,0},{4,5},{5,6},{6,7},{7,4},{8,9},{9,10},{10,1... | collective-permute-start | bytes 1572872 | tf_op jit(solution)/shard_map/ppermute | solution.py:15
  168.5 0.8 copy-start.14
  175.8 2.5 copy-start.18
  181.8 11.0 %copy-start.16 = (f32[1,128,128]{2,1,0:T(8,128)S(1)}, f32[1,128,128]{2,1,0:T(8,128)}, u32[]{:S(2)}) copy-start(f32[1,128,128]{2,1,0:T(8,128)} %param.26) | copy-start | bytes 196612
  181.9 23.8 %copy-start.9 = (bf16[1,32,128,128]{3,2,1,0:T(8,128)(2,1)S(1)}, bf16[1,32,128,128]{3,2,1,0:T(8,128)(2,1)}, u32[]{:S(2)}) copy-start(bf16[1,32,128,128]{3,2,1,0:T(8,128)(2,1)} %param.22) | copy-start | bytes 3145732
  198.9 11.1 %collective-permute-start.6 = (f32[4,128,128]{2,1,0:T(8,128)S(1)}, f32[4,128,128]{2,1,0:T(8,128)S(1)}, u32[]{:S(2)}, u32[]{:S(2)}) collective-permute-start(f32[4,128,128]{2,1,0:T(8,128)S(1)} %bitcast.119), channel_id=1, source_target_pairs={{0,8},{4,12},{8,16},{12,20},{16,24},{20,28},{24,0},{28,4},{1,9},{5... | collective-permute-start | bytes 786440 | tf_op jit(solution)/shard_map/ppermute | solution.py:15
  199.2 14.4 %collective-permute-start.7 = (f32[4,128,128]{2,1,0:T(8,128)S(1)}, f32[4,128,128]{2,1,0:T(8,128)S(1)}, u32[]{:S(2)}, u32[]{:S(2)}) collective-permute-start(f32[4,128,128]{2,1,0:T(8,128)S(1)} %bitcast.120), channel_id=1, source_target_pairs={{0,4},{4,8},{8,12},{12,16},{16,20},{20,24},{24,28},{28,0},{1,5},{5... | collective-permute-start | bytes 786440 | tf_op jit(solution)/shard_map/ppermute | solution.py:15
  199.7 14.3 %collective-permute-start.8 = (f32[4,128,128]{2,1,0:T(8,128)S(1)}, f32[4,128,128]{2,1,0:T(8,128)S(1)}, u32[]{:S(2)}, u32[]{:S(2)}) collective-permute-start(f32[4,128,128]{2,1,0:T(8,128)S(1)} %bitcast.121), channel_id=1, source_target_pairs={{0,28},{4,0},{8,4},{12,8},{16,12},{20,16},{24,20},{28,24},{1,29},{... | collective-permute-start | bytes 786440 | tf_op jit(solution)/shard_map/ppermute | solution.py:15
  204.0 16.6 %collective-permute-start.9 = (f32[4,128,128]{2,1,0:T(8,128)S(1)}, f32[4,128,128]{2,1,0:T(8,128)S(1)}, u32[]{:S(2)}, u32[]{:S(2)}) collective-permute-start(f32[4,128,128]{2,1,0:T(8,128)S(1)} %bitcast.122), channel_id=1, source_target_pairs={{0,24},{4,28},{8,0},{12,4},{16,8},{20,12},{24,16},{28,20},{1,25},{... | collective-permute-start | bytes 786440 | tf_op jit(solution)/shard_map/ppermute | solution.py:15
  213.7 8.4 %copy-start.13 = (f32[1,9,128,128]{3,2,1,0:T(8,128)S(1)}, f32[1,9,128,128]{3,2,1,0:T(8,128)}, u32[]{:S(2)}) copy-start(f32[1,9,128,128]{3,2,1,0:T(8,128)} %param.25) | copy-start | bytes 1769476
  228.9 3.1 %copy-start.6 = (f32[32,128,128]{2,1,0:T(8,128)S(1)}, f32[32,128,128]{2,1,0:T(8,128)}, u32[]{:S(2)}) copy-start(f32[32,128,128]{2,1,0:T(8,128)} %fusion.37) | copy-start | bytes 6291460
  245.9 13.9 %collective-permute-start.10 = (f32[1,128,1024]{2,1,0:T(8,128)S(1)}, f32[1,128,1024]{2,1,0:T(8,128)S(1)}, u32[]{:S(2)}, u32[]{:S(2)}) collective-permute-start(f32[1,128,1024]{2,1,0:T(8,128)S(1)} %copy.77), channel_id=1, source_target_pairs={{0,28},{4,0},{8,4},{12,8},{16,12},{20,16},{24,20},{28,24},{1,29},{... | collective-permute-start | bytes 1572872 | tf_op jit(solution)/shard_map/ppermute | solution.py:15
  246.2 13.7 %collective-permute-start.11 = (f32[1,128,1024]{2,1,0:T(8,128)S(1)}, f32[1,128,1024]{2,1,0:T(8,128)S(1)}, u32[]{:S(2)}, u32[]{:S(2)}) collective-permute-start(f32[1,128,1024]{2,1,0:T(8,128)S(1)} %copy.79), channel_id=1, source_target_pairs={{0,3},{1,0},{2,1},{3,2},{4,7},{5,4},{6,5},{7,6},{8,11},{9,8},{10,9... | collective-permute-start | bytes 1572872 | tf_op jit(solution)/shard_map/ppermute | solution.py:15
  260.0 0.8 copy-start.7
  260.1 0.9 copy-start.8
  299.0 3.6 %copy-start.21 = (f32[128]{0:T(128)}, f32[128]{0:T(128)S(1)}, u32[]{:S(2)}) copy-start(f32[128]{0:T(128)S(1)} %psum.15) | copy-start | bytes 1540
  299.0 3.6 %copy-start.1 = (bf16[1,96,128,128]{3,2,1,0:T(8,128)(2,1)S(1)}, bf16[1,96,128,128]{3,2,1,0:T(8,128)(2,1)}, u32[]{:S(2)}) copy-start(bf16[1,96,128,128]{3,2,1,0:T(8,128)(2,1)} %param.20) | copy-start | bytes 9437188
where the time goes:
time: 308 us; the launch traced here: 303 us
  matrix products  98.6 us (32%)
  blocking collectives  83.4 us (27%)
  waiting for transfers between devices  62.8 us (20%)
  local copies, waits for them, and re-layouts  27.9 us (9%)
  starting transfers between devices  15 us (5%)
  other arithmetic  13.8 us (4%)
    ppermute x12, waiting for transfers between devices, shifted(): return lax.ppermute(value, axis, pairs)  62.8 us
    psum x1, blocking collectives, shards(): lax.psum(jnp.sum(direction * image, axis=(0, 2)), ('sub', 'grp'))  39.5 us
    psum x1, blocking collectives, shards(): lax.psum(jnp.sum(new_residual * preconditioned, axis=(0, 2)), ('sub', 'gr...  38 us
    dot_general x1, matrix products, condensed(): jnp.einsum('lib,ibk->lik', paired, couple, precision=highest_precision)  21.7 us
    ppermute x12, starting transfers between devices, shifted(): return lax.ppermute(value, axis, pairs)  15 us
    dot_general x1, matrix products, precondition(): jnp.einsum('lcb,cb->lc', picked, primal_rows, precision=highest_precision)  11 us
    dot_general x2, matrix products, place_faces(): jnp.einsum('dk,dlf->lkf', slot_onehot, directed, precision=highest_precis...  9.93 us
    dot_general x1, matrix products, condensed(): jnp.einsum('lim,ikm->lik', middle, dirichlet, precision=highest_precision)  8.47 us
  transfers between devices with their start and end apart: 12, of which 8 were waited for; matrix products, arithmetic and copies ran while one was open for 2% of the time, Pallas kernels for 0%

commit v1 on v0

v1 whole, which is shorter than its diff:
```python
import functools

import jax
import jax.numpy as jnp
from jax import lax
from jax.experimental import pallas as pl
from jax.experimental.pallas import tpu as pltpu
from jax.sharding import PartitionSpec as P

REACH = 2
WINDOW = 2 * REACH + 1
MESH = pl.DeviceIdType.MESH
F32 = jnp.float32
BF16 = jnp.bfloat16
NN = (((1,), (0,)), ((), ()))
NT = (((1,), (1,)), ((), ()))


def split(value):
    high = value.astype(BF16)
    low = (value - high.astype(F32)).astype(BF16)
    return jnp.concatenate([high, low], 0)


def merge(value):
    half = value.shape[0] // 2
    return value[:half] + value[half:]


def dot(lhs, rhs, dims=NN):
    return lax.dot_general(lhs, rhs, dims, preferred_element_type=F32)


def exact(lhs, rhs):
    return lax.dot_general(
        lhs, rhs, NN, preferred_element_type=F32, precision=lax.Precision.HIGHEST
    )


def row_sums(value):
    return jnp.sum(value.T, axis=0, keepdims=True)


def as_columns(row, width):
    return jnp.broadcast_to(row, (width, row.shape[1])).T


def kernel(
    n_sub, n_grp,
    sol_h, res_h, dir_h, rp_ref, slots, coup_h, diri_h, face_h, neum_h, pb_ref, basis_h,
    cmat_h, cinv_h, pattern,
    osol_h, ores_h, odir_h, oprod,
    inv_s, U, R, Uhl, V, B, Y, RY, Hhl, H, LS, RLS, S, OD, Cw, Fd, Fb, Nf, basis, basisx,
    cmat, cinv, Wn, acc, cr2, RB, RP, SP, RC, corr, red_g, red_s, red_g2, red_s2, crs,
    stepb, csem, snd, rcv,
):
    ms = lax.axis_index("sub")
    mg = lax.axis_index("grp")
    width = basis.shape[0]
    nb = Fb.shape[0]
    fb = nb // 4
    n_q = Cw.shape[0] // nb
    counter = [0]
    pending = []

    def sub_at(offset):
        return (lax.rem(ms + offset + n_sub, n_sub), mg)

    def grp_at(offset):
        return (ms, lax.rem(mg + offset + n_grp, n_grp))

    def send(src, dst, device):
        i = counter[0]
        counter[0] += 1
        copy = pltpu.make_async_remote_copy(
            src_ref=src, dst_ref=dst, send_sem=snd.at[i], recv_sem=rcv.at[i],
            device_id=device, device_id_type=MESH,
        )
        copy.start()
        pending.append(copy)
        return copy

    def blocks(ref, d):
        return ref.at[pl.ds(d * fb, fb)]

    def columns(ref, half, k):
        return ref.at[0, :, pl.ds((half * fb + k) * width, width)]

    def fetch_face(hbm, half, buf, d, sem):
        for k in range(fb):
            pltpu.make_async_copy(columns(hbm, half, k), buf.at[d * fb + k], csem.at[sem]).start()

    def wait_face(buf, d, sem):
        pltpu.make_async_copy(blocks(buf, d), blocks(buf, d), csem.at[sem]).wait()

    def store_face(buf, d, hbm, half, sem):
        for k in range(fb):
            pltpu.make_async_copy(buf.at[d * fb + k], columns(hbm, half, k), csem.at[sem]).start()

    fetch_face(dir_h, 0, U, 1, 0)
    fetch_face(dir_h, 1, U, 3, 1)
    weight_copies = []
    for s in range(4):
        group = []
        for q in range(n_q):
            part = pl.ds(q * nb + s * fb, fb)
            group.append(pltpu.make_async_copy(coup_h.at[0, part], Cw.at[part], csem.at[10 + 7 * s + q]))
            group.append(pltpu.make_async_copy(diri_h.at[0, part], Fd.at[part], csem.at[10 + 7 * s + 3 + q]))
        part = pl.ds(s * fb, fb)
        group.append(pltpu.make_async_copy(face_h.at[0, part], Fb.at[part], csem.at[10 + 7 * s + 6]))
        weight_copies.append(group)

    barrier = pltpu.get_barrier_semaphore()
    for o in range(1, n_sub):
        pl.semaphore_signal(barrier, inc=1, device_id=sub_at(o), device_id_type=MESH)
    for o in range(1, n_grp):
        pl.semaphore_signal(barrier, inc=1, device_id=grp_at(o), device_id_type=MESH)
    for c in weight_copies[0]:
        c.start()
    fetch_face(res_h, 0, R, 1, 2)
    fetch_face(res_h, 1, R, 3, 3)
    small = [
        pltpu.make_async_copy(basis_h.at[0], basis, csem.at[4]),
        pltpu.make_async_copy(cmat_h.at[0], cmat, csem.at[5]),
        pltpu.make_async_copy(cinv_h.at[0], cinv, csem.at[6]),
        pltpu.make_async_copy(neum_h.at[0], Nf, csem.at[7]),
    ]
    small[0].start()
    for group in weight_copies[1:]:
        for c in group:
            c.start()
    for c in small[1:]:
        c.start()
    fetch_face(sol_h, 0, S, 0, 8)
    fetch_face(sol_h, 1, S, 1, 9)
    pl.semaphore_wait(barrier, n_sub + n_grp - 2)

    wait_face(U, 1, 0)
    u_sub = send(blocks(U, 1), blocks(U, 0), sub_at(1))
    wait_face(U, 3, 1)
    u_grp = send(blocks(U, 3), blocks(U, 2), grp_at(1))
    wait_face(R, 1, 2)
    r_sub = send(blocks(R, 1), blocks(R, 0), sub_at(1))
    wait_face(R, 3, 3)
    r_grp = send(blocks(R, 3), blocks(R, 2), grp_at(1))

    small[0].wait()
    basisx[...] = basis[...].astype(F32)
    primal = pb_ref[...].astype(F32)
    for side in range(2):
        SP[side] = primal - (slots[0, 2 * side] * fb).astype(F32)
    extra = []
    for side, device in ((0, sub_at(-1)), (1, grp_at(-1))):
        extra.append(send(basisx, RB.at[side], device))
        extra.append(send(SP.at[side], RP.at[side], device))

    for s in range(4):
        at = jnp.int32(0)
        for d in range(4):
            at = jnp.where(slots[0, d] == s, jnp.int32(d * fb), at)
        inv_s[s] = at
    acc[...] = jnp.zeros_like(acc)

    u_grp.wait_recv()
    u_sub.wait_recv()

    for s in range(4):
        def prepare(k, carry, s=s):
            Uhl[s * fb + k] = split(U[inv_s[s] + k])
            return carry
        lax.fori_loop(0, fb, prepare, 0, unroll=2)

    for s in range(4):
        for c in weight_copies[s]:
            c.wait()

        def interior(k, carry, s=s):
            j = s * fb + k
            uj = Uhl[j]
            v = merge(dot(uj, Fb[j]))
            V[j] = v
            total = U[inv_s[s] + k] * v
            for q in range(n_q):
                m = lax.rem(j + q + 1, nb)
                n = q * nb + j
                a = merge(dot(jnp.concatenate([uj, Uhl[m]], 1), Cw[n]))
                t = merge(dot(split(a), Fd[n]))
                total = total + t * t
                B[n] = split(merge(dot(split(t), Fd[n], NT)))
            acc[...] += total
            return carry
        lax.fori_loop(0, fb, interior, 0, unroll=2)

    def reduce_start(row, red, first, index, count, at):
        red[index] = row
        return [send(red.at[index], red.at[index], at(o)) for o in range(1, count)]

    def reduce_end(copies, red, count):
        for c in copies:
            c.wait_recv()
        for c in copies:
            c.wait_send()
            pending[:] = [other for other in pending if other is not c]
        total = red[0]
        for i in range(1, count):
            total = total + red[i]
        return total

    copies = reduce_start(row_sums(acc[...]), red_g, True, mg, n_grp, grp_at)

    def returned(d):
        def body(k, carry):
            j = slots[0, d] * fb + k
            lhs = []
            rhs = []
            for q in range(n_q):
                n = q * nb + j
                p = q * nb + lax.rem(j - q - 1 + nb, nb)
                lhs += [B[n], B[p]]
                rhs += [Cw[n, :width], Cw[p, width:]]
            y = merge(dot(jnp.concatenate(lhs, 1), jnp.concatenate(rhs, 1), NT))
            Y[d * fb + k] = y + V[j]
            return carry
        lax.fori_loop(0, fb, body, 0, unroll=2)

    returned(0)
    part = reduce_end(copies, red_g, n_grp)
    copies = reduce_start(part, red_s, True, ms, n_sub, sub_at)
    ys = {}
    ys[1] = send(blocks(Y, 0), blocks(RY, 1), sub_at(-1))
    returned(1)
    ys[0] = send(blocks(Y, 1), blocks(RY, 0), sub_at(1))
    returned(2)
    ys[3] = send(blocks(Y, 2), blocks(RY, 3), grp_at(-1))
    returned(3)
    ys[2] = send(blocks(Y, 3), blocks(RY, 2), grp_at(1))
    curvature = reduce_end(copies, red_s, n_sub)
    rp = rp_ref[...]
    stepb[...] = as_columns(rp / curvature, width)

    wait_face(S, 0, 8)
    wait_face(S, 1, 9)
    for half in range(2):
        def iterate(k, carry, half=half):
            S[half * fb + k] = S[half * fb + k] + stepb[...] * U[(2 * half + 1) * fb + k]
            return carry
        lax.fori_loop(0, fb, iterate, 0, unroll=2)
        store_face(S, half, osol_h, half, 8 + half)

    for c in extra:
        c.wait_recv()
    r_grp.wait_recv()
    r_sub.wait_recv()
    for c in small[1:]:
        c.wait()
    pbc = as_columns(primal, width)
    cr2[...] = jnp.zeros_like(cr2)
    acc[...] = jnp.zeros_like(acc)
    basis32 = basisx[...]

    def pick(j):
        return jnp.where(pbc == j.astype(F32), basis32, 0.0).astype(BF16)

    def residual_face(d):
        ys[d].wait_recv()

        def body(k, carry):
            i = d * fb + k
            new = R[i] - stepb[...] * (Y[i] + RY[i])
            H[i] = new
            hl = split(new * 0.5)
            Hhl[i] = hl
            cr2[...] += dot(hl, pick(slots[0, d] * fb + k), NT)
            return carry
        lax.fori_loop(0, fb, body, 0, unroll=2)
        if d % 2 == 1:
            store_face(H, d, ores_h, d // 2, d - 1 - d // 2)

    def local_face(d):
        def body(k, carry):
            i = d * fb + k
            factor = Nf[slots[0, d] * fb + k]
            t = merge(dot(Hhl[i], factor))
            acc[...] += t * t
            LS[i] = 0.5 * merge(dot(split(t), factor, NT))
            return carry
        lax.fori_loop(0, fb, body, 0, unroll=2)

    residual_face(2)
    local_face(2)
    ls_grp = send(blocks(LS, 2), blocks(RLS, 1), grp_at(-1))
    residual_face(3)
    local_face(3)
    residual_face(1)
    residual_face(0)
    cr = merge(cr2[...])
    crs[...] = cr
    first = exact(cr, cinv[...])

    def place(g, p):
        return Wn.at[g * WINDOW + p]

    Wn[mg * WINDOW + REACH] = first
    arrivals = {}
    for o in (1, -1, 2, -2):
        p = REACH - o
        arrivals[p] = send(place(mg, REACH), place(mg, p), sub_at(o))
    order = (REACH, REACH - 2, REACH + 2, REACH - 1, REACH + 1)
    if n_grp == 4:
        near = (ms, mg + 1 - 2 * lax.rem(mg, 2))
        far = lax.rem(mg + 2, 4)
        far_copies = {}
        column_copies = []

        def pass_on(p):
            far_copies[p] = send(place(mg, p), place(mg, p), (ms, far))
            column_copies.append(send(place(mg, p), place(mg, p), near))
        pass_on(REACH)
        local_face(0)
        ls_sub = send(blocks(LS, 0), blocks(RLS, 0), sub_at(-1))
        for p in order[1:]:
            arrivals[p].wait_recv()
            pass_on(p)
        local_face(1)
        for p in order:
            far_copies[p].wait_recv()
            column_copies.append(send(place(far, p), place(far, p), near))
        for c in column_copies:
            c.wait_recv()
    else:
        column_copies = []
        local_face(0)
        ls_sub = send(blocks(LS, 0), blocks(RLS, 0), sub_at(-1))
        for p in order:
            if p != REACH:
                arrivals[p].wait_recv()
            for o in range(1, n_grp):
                column_copies.append(send(place(mg, p), place(mg, p), grp_at(o)))
        local_face(1)
        for c in column_copies:
            c.wait_recv()

    chosen = []
    for k in range(cmat.shape[0]):
        entry = pattern[0, k]
        p = lax.min(lax.rem(entry // n_grp - ms + REACH + n_sub, n_sub), jnp.int32(WINDOW - 1))
        chosen.append(Wn[lax.rem(entry, n_grp) * WINDOW + p])
    adjacent = exact(
        jnp.concatenate(chosen, 1), cmat[...].reshape(cmat.shape[0] * width, width)
    )
    correction = Wn[mg * WINDOW + REACH] + exact(crs[...] - adjacent, cinv[...])
    corr[...] = correction
    c_sub = send(corr, RC.at[0], sub_at(-1))
    c_grp = send(corr, RC.at[1], grp_at(-1))
    product_row = row_sums(acc[...] + correction * crs[...])
    copies = reduce_start(product_row, red_g2, False, mg, n_grp, grp_at)

    corr_hl = split(correction * 0.5)

    def own_spread(d):
        def body(k, carry):
            i = d * fb + k
            LS[i] = LS[i] + merge(dot(corr_hl, pick(slots[0, d] * fb + k)))
            return carry
        lax.fori_loop(0, fb, body, 0, unroll=2)

    own_spread(1)
    part = reduce_end(copies, red_g2, n_grp)
    copies = reduce_start(part, red_s2, False, ms, n_sub, sub_at)
    own_spread(3)

    def borrowed_spread(side):
        d = 2 * side + 1
        relative = as_columns(RP[side], width)
        other = RB[side]
        other_hl = split(RC[side] * 0.5)

        def body(k, carry):
            i = d * fb + k
            rows = jnp.where(relative == k.astype(F32), other, 0.0).astype(BF16)
            OD[side * fb + k] = LS[i] + RLS[side * fb + k] + merge(dot(other_hl, rows))
            return carry
        lax.fori_loop(0, fb, body, 0, unroll=2)

    ls_grp.wait_recv()
    c_grp.wait_recv()
    borrowed_spread(1)
    ls_sub.wait_recv()
    c_sub.wait_recv()
    borrowed_spread(0)
    product = reduce_end(copies, red_s2, n_sub)
    oprod[...] = product
    ratio = as_columns(product / rp, width)
    for half in range(2):
        def advance(k, carry, half=half):
            OD[half * fb + k] = OD[half * fb + k] + ratio * U[(2 * half + 1) * fb + k]
            return carry
        lax.fori_loop(0, fb, advance, 0, unroll=2)
        store_face(OD, half, odir_h, half, 2 + half)

    for half in range(2):
        wait_face(S, half, 8 + half)
        wait_face(H, 2 * half + 1, half)
        wait_face(OD, half, 2 + half)
    for c in pending:
        c.wait_send()


def shards(
    solution, residual, direction, residual_product, neighbor_slots, coupling,
    dirichlet_factor, face_block, neumann_factor, primal_block, primal_basis,
    coarse_matrix, coarse_block_inverse, coarse_pattern,
):
    n_sub = lax.axis_size("sub")
    n_grp = lax.axis_size("grp")
    loads = direction.shape[1]
    nb = face_block.shape[1]
    width = face_block.shape[2]
    fb = nb // 4
    inner = coupling.shape[1]
    copies = 8 + 4 + 2 + 2 + 4 + 3 * WINDOW + 2 * (n_sub + n_grp) + WINDOW * n_grp
    hbm = pl.BlockSpec(memory_space=pl.ANY)
    vmem = pl.BlockSpec(memory_space=pltpu.VMEM)
    smem = pl.BlockSpec(memory_space=pltpu.SMEM)

    def block(count, dtype=F32, rows=loads):
        return pltpu.VMEM((count, rows, width), dtype)

    scratch = [
        pltpu.SMEM((4,), jnp.int32),
        block(nb), block(nb), block(nb, BF16, 2 * loads), block(nb),
        block(inner, BF16, 2 * loads), block(nb), block(nb),
        block(nb, BF16, 2 * loads), block(nb), block(nb), block(2 * fb), block(2 * fb),
        block(2 * fb),
        pltpu.VMEM(coupling.shape[1:], BF16), pltpu.VMEM(dirichlet_factor.shape[1:], BF16),
        pltpu.VMEM(face_block.shape[1:], BF16), pltpu.VMEM(neumann_factor.shape[1:], BF16),
        pltpu.VMEM(primal_basis.shape[1:], BF16), pltpu.VMEM(primal_basis.shape[1:], F32),
        pltpu.VMEM(coarse_matrix.shape[1:], F32), pltpu.VMEM(coarse_block_inverse.shape[1:], F32),
        block(n_grp * WINDOW),
        pltpu.VMEM((loads, width), F32),
        pltpu.VMEM((2 * loads, width), F32),
        block(2), pltpu.VMEM((2, 1, width), F32), pltpu.VMEM((2, 1, width), F32),
        block(2), pltpu.VMEM((loads, width), F32),
        pltpu.VMEM((n_grp, 1, loads), F32), pltpu.VMEM((n_sub, 1, loads), F32),
        pltpu.VMEM((n_grp, 1, loads), F32), pltpu.VMEM((n_sub, 1, loads), F32),
        pltpu.VMEM((loads, width), F32), pltpu.VMEM((loads, width), F32),
        pltpu.SemaphoreType.DMA((40,)),
        pltpu.SemaphoreType.DMA((copies,)), pltpu.SemaphoreType.DMA((copies,)),
    ]
    field = jax.ShapeDtypeStruct(solution.shape, F32)
    outs = pl.pallas_call(
        functools.partial(kernel, n_sub, n_grp),
        out_shape=(field, field, field, jax.ShapeDtypeStruct((1, loads), F32)),
        in_specs=[hbm, hbm, hbm, vmem, smem, hbm, hbm, hbm, hbm, vmem, hbm, hbm, hbm, smem],
        out_specs=(hbm, hbm, hbm, vmem),
        scratch_shapes=scratch,
        compiler_params=pltpu.CompilerParams(
            collective_id=0, has_side_effects=True, vmem_limit_bytes=58 * 1024 * 1024
        ),
    )(
        solution, residual, direction, residual_product.reshape(1, -1), neighbor_slots,
        coupling, dirichlet_factor, face_block, neumann_factor, primal_block, primal_basis,
        coarse_matrix, coarse_block_inverse, coarse_pattern,
    )
    return outs[0], outs[1], outs[2], outs[3].reshape(-1)


def solution(mesh):
    rows = P(("sub", "grp"))
    in_specs = (rows, rows, rows, P()) + (rows,) * 10
    out_specs = (rows, rows, rows, P())
    return jax.shard_map(shards, mesh=mesh, in_specs=in_specs, out_specs=out_specs, check_vma=False)
```

time: 308 us -> 107 us (0.35); the launches traced: 303 us -> 106 us
  matrix products: 98.6 us -> 0 us
  Pallas kernels: 0 us -> 98.4 us
  blocking collectives: 83.4 us -> 0 us
  waiting for transfers between devices: 62.8 us -> 0 us
  local copies, waits for them, and re-layouts: 27.9 us -> 7.4 us
  starting transfers between devices: 15 us -> 0 us
  other arithmetic: 13.8 us -> 0 us
    dot_general x18 -> x0, matrix products: 98.6 us -> none  [the longest x1 21.7 us: condensed(): jnp.einsum('lib,ibk->lik', paired, couple, precision=highest_precision)]
    pallas_call x0 -> x1, Pallas kernels: none -> 98.4 us  [shards(): pl.pallas_call(functools.partial(kernel, n_sub, n_grp), out_shape=(field,...]
    psum x2 -> x0, blocking collectives: 77.6 us -> none  [the longest x1 39.5 us: shards(): lax.psum(jnp.sum(direction * image, axis=(0, 2)), ('sub', 'grp'))]
    ppermute x12 -> x0, waiting for transfers between devices: 62.8 us -> none  [shifted(): return lax.ppermute(value, axis, pairs)]
    ppermute x12 -> x0, starting transfers between devices: 15 us -> none  [shifted(): return lax.ppermute(value, axis, pairs)]
    reshape x3 -> x0, local copies, waits for them, and re-layouts: 9.42 us -> none  [the longest x2 6.38 us: collect(): placed = local_part.reshape(load_count, 4, -1)]
    slice x16 -> x0, local copies, waits for them, and re-layouts: 7.98 us -> none  [the longest x2 3.06 us: collect(): owned_sub = directed[1][None] + to_sub]
    concatenate x1 -> x0, other arithmetic: 6.13 us -> none  [condensed(): jnp.concatenate([jnp.concatenate([vector, jnp.roll(vector, -(offset + 1),...]
  transfers between devices with their start and end apart: 12 -> 0, of which waited for: 8 -> 0; matrix products, arithmetic and copies ran while one was open for 2% -> 0% of each run, Pallas kernels for 0% -> 0%
where the time goes in v1:
time: 107 us; the launch traced here: 106 us
  Pallas kernels  98.4 us (92%)
  local copies, waits for them, and re-layouts  7.4 us (7%)
    pallas_call x1, Pallas kernels, shards(): pl.pallas_call(functools.partial(kernel, n_sub, n_grp), out_shape=(field,...  98.4 us
    unnamed x6, local copies, waits for them, and re-layouts  7.4 us

profile of v1, /device:TPU:0, one launch (start us, length us, event | category | flops | bytes accessed | tf_op | source)
XLA Modules:
  0.0 106.5 jit_solution(4671435690842477237)
XLA Ops:
  0.6 98.4 %shard_map.165 = (f32[1,128,2048]{2,1,0:T(8,128)}, f32[1,128,2048]{2,1,0:T(8,128)}, f32[1,128,2048]{2,1,0:T(8,128)}, f32[1,128]{1,0:T(1,128)}) custom-call(f32[1,128,2048]{2,1,0:T(8,128)} %sol_h.1, f32[1,128,2048]{2,1,0:T(8,128)} %res_h.1, f32[1,128,2048]{2,1,0:T(8,128)} %dir_h.1, f32[1,128]{1,0:T(1,128)} %bitcast.2, s32[1,4]{1,0:T(1,128)} %slots.1, ...), custom_call_target="tpu_custom_call" | custom-call | tf_op jit(solution)/shard_map/pallas_call | solution.py:451
  99.1 0.0 copy-start
  99.1 2.3 %copy.22 = f32[1,128,2048]{2,1,0:T(8,128)} copy(f32[1,128,2048]{2,1,0:T(8,128)} %get-tuple-element.16) | data formatting | bytes 2097152
  101.4 2.3 %copy.23 = f32[1,128,2048]{2,1,0:T(8,128)} copy(f32[1,128,2048]{2,1,0:T(8,128)} %get-tuple-element.17) | data formatting | bytes 2097152
  103.7 2.3 %copy.24 = f32[1,128,2048]{2,1,0:T(8,128)} copy(f32[1,128,2048]{2,1,0:T(8,128)} %get-tuple-element.18) | data formatting | bytes 2097152
  106.0 0.0 copy-done
  106.0 0.5 copy.25
Async XLA Ops:
  99.1 6.9 %copy-start = (f32[1,128]{1,0:T(1,128)S(1)}, f32[1,128]{1,0:T(1,128)}, u32[]{:S(2)}) copy-start(f32[1,128]{1,0:T(1,128)} %get-tuple-element.11) | copy-start | bytes 1540

commit v2 on v1

--- a/solution.py
+++ b/solution.py
@@ -50,8 +50,8 @@
     sol_h, res_h, dir_h, rp_ref, slots, coup_h, diri_h, face_h, neum_h, pb_ref, basis_h,
     cmat_h, cinv_h, pattern,
     osol_h, ores_h, odir_h, oprod,
-    inv_s, U, R, Uhl, V, B, Y, RY, Hhl, H, LS, RLS, S, OD, Cw, Fd, Fb, Nf, basis, basisx,
-    cmat, cinv, Wn, acc, cr2, RB, RP, SP, RC, corr, red_g, red_s, red_g2, red_s2, crs,
+    inv_s, U, R, Uhl, V, B, Y, RY, Hhl, H, LS, NXs, NXr, S, OD, Cw, Fd, Fb, Nf, basis, basisx,
+    cmat, cinv, Wn, acc, cr2, crn2, crn, rcr, rel, RB, RP, SP, RC, corr, red_g, red_s, red_g2, red_s2, crs,
     stepb, csem, snd, rcv,
 ):
     ms = lax.axis_index("sub")
@@ -126,10 +126,11 @@
         pltpu.make_async_copy(neum_h.at[0], Nf, csem.at[7]),
     ]
     small[0].start()
+    small[3].start()
     for group in weight_copies[1:]:
         for c in group:
             c.start()
-    for c in small[1:]:
+    for c in small[1:3]:
         c.start()
     fetch_face(sol_h, 0, S, 0, 8)
     fetch_face(sol_h, 1, S, 1, 9)
@@ -139,21 +140,18 @@
     u_sub = send(blocks(U, 1), blocks(U, 0), sub_at(1))
     wait_face(U, 3, 1)
     u_grp = send(blocks(U, 3), blocks(U, 2), grp_at(1))
-    wait_face(R, 1, 2)
-    r_sub = send(blocks(R, 1), blocks(R, 0), sub_at(1))
-    wait_face(R, 3, 3)
-    r_grp = send(blocks(R, 3), blocks(R, 2), grp_at(1))
+    small[3].wait()
+    for side in range(2):
+        def widen(k, carry, side=side):
+            NXs[side * fb + k] = Nf[slots[0, 2 * side] * fb + k].astype(F32)
+            return carry
+        lax.fori_loop(0, fb, widen, 0, unroll=2)
 
     small[0].wait()
     basisx[...] = basis[...].astype(F32)
     primal = pb_ref[...].astype(F32)
     for side in range(2):
         SP[side] = primal - (slots[0, 2 * side] * fb).astype(F32)
-    extra = []
-    for side, device in ((0, sub_at(-1)), (1, grp_at(-1))):
-        extra.append(send(basisx, RB.at[side], device))
-        extra.append(send(SP.at[side], RP.at[side], device))
-
     for s in range(4):
         at = jnp.int32(0)
         for d in range(4):
@@ -163,6 +161,11 @@
 
     u_grp.wait_recv()
     u_sub.wait_recv()
+    extra = []
+    for side, device in ((0, sub_at(-1)), (1, grp_at(-1))):
+        extra.append(send(blocks(NXs, side), blocks(NXr, side), device))
+        extra.append(send(basisx, RB.at[side], device))
+        extra.append(send(SP.at[side], RP.at[side], device))
 
     for s in range(4):
         def prepare(k, carry, s=s):
@@ -228,12 +231,10 @@
     copies = reduce_start(part, red_s, True, ms, n_sub, sub_at)
     ys = {}
     ys[1] = send(blocks(Y, 0), blocks(RY, 1), sub_at(-1))
-    returned(1)
-    ys[0] = send(blocks(Y, 1), blocks(RY, 0), sub_at(1))
     returned(2)
     ys[3] = send(blocks(Y, 2), blocks(RY, 3), grp_at(-1))
+    returned(1)
     returned(3)
-    ys[2] = send(blocks(Y, 3), blocks(RY, 2), grp_at(1))
     curvature = reduce_end(copies, red_s, n_sub)
     rp = rp_ref[...]
     stepb[...] = as_columns(rp / curvature, width)
@@ -249,10 +250,12 @@
 
     for c in extra:
         c.wait_recv()
-    r_grp.wait_recv()
-    r_sub.wait_recv()
-    for c in small[1:]:
+    for c in small[1:3]:
         c.wait()
+    wait_face(R, 1, 2)
+    wait_face(R, 3, 3)
+    for side in range(2):
+        rel[side] = as_columns(RP[side], width)
     pbc = as_columns(primal, width)
     cr2[...] = jnp.zeros_like(cr2)
     acc[...] = jnp.zeros_like(acc)
@@ -261,8 +264,13 @@
     def pick(j):
         return jnp.where(pbc == j.astype(F32), basis32, 0.0).astype(BF16)
 
+    def pick_other(side, k):
+        return jnp.where(rel[side] == k.astype(F32), RB[side], 0.0).astype(BF16)
+
     def residual_face(d):
+        side = d // 2
         ys[d].wait_recv()
+        crn2[...] = jnp.zeros_like(crn2)
 
         def body(k, carry):
             i = d * fb + k
@@ -271,29 +279,35 @@
             hl = split(new * 0.5)
             Hhl[i] = hl
             cr2[...] += dot(hl, pick(slots[0, d] * fb + k), NT)
+            crn2[...] += dot(hl, pick_other(side, k), NT)
             return carry
         lax.fori_loop(0, fb, body, 0, unroll=2)
-        if d % 2 == 1:
-            store_face(H, d, ores_h, d // 2, d - 1 - d // 2)
+        crn[side] = merge(crn2[...])
+        store_face(H, d, ores_h, side, side)
 
     def local_face(d):
+        side = d // 2
+
         def body(k, carry):
             i = d * fb + k
+            hl = Hhl[i]
             factor = Nf[slots[0, d] * fb + k]
-            t = merge(dot(Hhl[i], factor))
-            acc[...] += t * t
-            LS[i] = 0.5 * merge(dot(split(t), factor, NT))
+            other = NXr[side * fb + k].astype(BF16)
+            t = merge(dot(hl, factor))
+            w = merge(dot(hl, other))
+            acc[...] += t * t + w * w
+            LS[i] = 0.5 * (merge(dot(split(t), factor, NT)) + merge(dot(split(w), other, NT)))
             return carry
         lax.fori_loop(0, fb, body, 0, unroll=2)
 
-    residual_face(2)
-    local_face(2)
-    ls_grp = send(blocks(LS, 2), blocks(RLS, 1), grp_at(-1))
     residual_face(3)
+    cr_grp = send(crn.at[1], rcr.at[1], grp_at(1))
+    residual_face(1)
+    cr_sub = send(crn.at[0], rcr.at[0], sub_at(1))
     local_face(3)
-    residual_face(1)
-    residual_face(0)
-    cr = merge(cr2[...])
+    cr_grp.wait_recv()
+    cr_sub.wait_recv()
+    cr = merge(cr2[...]) + rcr[0] + rcr[1]
     crs[...] = cr
     first = exact(cr, cinv[...])
 
@@ -316,12 +330,10 @@
             far_copies[p] = send(place(mg, p), place(mg, p), (ms, far))
             column_copies.append(send(place(mg, p), place(mg, p), near))
         pass_on(REACH)
-        local_face(0)
-        ls_sub = send(blocks(LS, 0), blocks(RLS, 0), sub_at(-1))
+        local_face(1)
         for p in order[1:]:
             arrivals[p].wait_recv()
             pass_on(p)
-        local_face(1)
         for p in order:
             far_copies[p].wait_recv()
             column_copies.append(send(place(far, p), place(far, p), near))
@@ -329,14 +341,12 @@
             c.wait_recv()
     else:
         column_copies = []
-        local_face(0)
-        ls_sub = send(blocks(LS, 0), blocks(RLS, 0), sub_at(-1))
+        local_face(1)
         for p in order:
             if p != REACH:
                 arrivals[p].wait_recv()
             for o in range(1, n_grp):
                 column_copies.append(send(place(mg, p), place(mg, p), grp_at(o)))
-        local_face(1)
         for c in column_copies:
             c.wait_recv()
 
@@ -371,21 +381,17 @@
 
     def borrowed_spread(side):
         d = 2 * side + 1
-        relative = as_columns(RP[side], width)
-        other = RB[side]
         other_hl = split(RC[side] * 0.5)
 
         def body(k, carry):
             i = d * fb + k
-            rows = jnp.where(relative == k.astype(F32), other, 0.0).astype(BF16)
-            OD[side * fb + k] = LS[i] + RLS[side * fb + k] + merge(dot(other_hl, rows))
+            rows = pick_other(side, k)
+            OD[side * fb + k] = LS[i] + merge(dot(other_hl, rows))
             return carry
         lax.fori_loop(0, fb, body, 0, unroll=2)
 
-    ls_grp.wait_recv()
     c_grp.wait_recv()
     borrowed_spread(1)
-    ls_sub.wait_recv()
     c_sub.wait_recv()
     borrowed_spread(0)
     product = reduce_end(copies, red_s2, n_sub)
@@ -419,7 +425,8 @@
     fb = nb // 4
     inner = coupling.shape[1]
     copies = 8 + 4 + 2 + 2 + 4 + 3 * WINDOW + 2 * (n_sub + n_grp) + WINDOW * n_grp
-    hbm = pl.BlockSpec(memory_space=pl.ANY)
+    hbm = pl.BlockSpec(memory_space=pltpu.HBM)
+    free = pl.BlockSpec(memory_space=pl.ANY)
     vmem = pl.BlockSpec(memory_space=pltpu.VMEM)
     smem = pl.BlockSpec(memory_space=pltpu.SMEM)
 
@@ -431,15 +438,15 @@
         block(nb), block(nb), block(nb, BF16, 2 * loads), block(nb),
         block(inner, BF16, 2 * loads), block(nb), block(nb),
         block(nb, BF16, 2 * loads), block(nb), block(nb), block(2 * fb), block(2 * fb),
-        block(2 * fb),
+        block(2 * fb), block(2 * fb),
         pltpu.VMEM(coupling.shape[1:], BF16), pltpu.VMEM(dirichlet_factor.shape[1:], BF16),
         pltpu.VMEM(face_block.shape[1:], BF16), pltpu.VMEM(neumann_factor.shape[1:], BF16),
         pltpu.VMEM(primal_basis.shape[1:], BF16), pltpu.VMEM(primal_basis.shape[1:], F32),
         pltpu.VMEM(coarse_matrix.shape[1:], F32), pltpu.VMEM(coarse_block_inverse.shape[1:], F32),
         block(n_grp * WINDOW),
         pltpu.VMEM((loads, width), F32),
-        pltpu.VMEM((2 * loads, width), F32),
-        block(2), pltpu.VMEM((2, 1, width), F32), pltpu.VMEM((2, 1, width), F32),
+        pltpu.VMEM((2 * loads, width), F32), pltpu.VMEM((2 * loads, width), F32),
+        block(2), block(2), block(2), block(2), pltpu.VMEM((2, 1, width), F32), pltpu.VMEM((2, 1, width), F32),
         block(2), pltpu.VMEM((loads, width), F32),
         pltpu.VMEM((n_grp, 1, loads), F32), pltpu.VMEM((n_sub, 1, loads), F32),
         pltpu.VMEM((n_grp, 1, loads), F32), pltpu.VMEM((n_sub, 1, loads), F32),
@@ -452,10 +459,10 @@
         functools.partial(kernel, n_sub, n_grp),
         out_shape=(field, field, field, jax.ShapeDtypeStruct((1, loads), F32)),
         in_specs=[hbm, hbm, hbm, vmem, smem, hbm, hbm, hbm, hbm, vmem, hbm, hbm, hbm, smem],
-        out_specs=(hbm, hbm, hbm, vmem),
+        out_specs=(free, free, free, vmem),
         scratch_shapes=scratch,
         compiler_params=pltpu.CompilerParams(
-            collective_id=0, has_side_effects=True, vmem_limit_bytes=58 * 1024 * 1024
+            collective_id=0, has_side_effects=True, vmem_limit_bytes=62 * 1024 * 1024
         ),
     )(
         solution, residual, direction, residual_product.reshape(1, -1), neighbor_slots,

time: 107 us -> 97.4 us (0.910)
  Pallas kernels: 98.4 us -> 89.1 us
    pallas_call x1, Pallas kernels: 98.4 us -> 89.1 us  [shards(): pl.pallas_call(functools.partial(kernel, n_sub, n_grp), out_shape=(field,...]
where the time goes in v2:
time: 97.4 us; the launch traced here: 97.1 us
  Pallas kernels  89.1 us (91%)
  local copies, waits for them, and re-layouts  7.4 us (8%)
    pallas_call x1, Pallas kernels, shards(): pl.pallas_call(functools.partial(kernel, n_sub, n_grp), out_shape=(field,...  89.1 us
    unnamed x6, local copies, waits for them, and re-layouts  7.4 us

profile of v2, /device:TPU:0, one launch (start us, length us, event | category | flops | bytes accessed | tf_op | source)
XLA Modules:
  0.0 97.1 jit_solution(6208284556872000532)
XLA Ops:
  0.6 89.1 %shard_map.165 = (f32[1,128,2048]{2,1,0:T(8,128)}, f32[1,128,2048]{2,1,0:T(8,128)}, f32[1,128,2048]{2,1,0:T(8,128)}, f32[1,128]{1,0:T(1,128)}) custom-call(f32[1,128,2048]{2,1,0:T(8,128)} %sol_h.1, f32[1,128,2048]{2,1,0:T(8,128)} %res_h.1, f32[1,128,2048]{2,1,0:T(8,128)} %dir_h.1, f32[1,128]{1,0:T(1,128)} %bitcast.2, s32[1,4]{1,0:T(1,128)} %slots.1, ...), custom_call_target="tpu_custom_call" | custom-call | tf_op jit(solution)/shard_map/pallas_call | solution.py:458
  89.7 0.0 copy-start
  89.7 2.3 %copy.22 = f32[1,128,2048]{2,1,0:T(8,128)} copy(f32[1,128,2048]{2,1,0:T(8,128)} %get-tuple-element.16) | data formatting | bytes 2097152
  92.0 2.3 %copy.23 = f32[1,128,2048]{2,1,0:T(8,128)} copy(f32[1,128,2048]{2,1,0:T(8,128)} %get-tuple-element.17) | data formatting | bytes 2097152
  94.3 2.3 %copy.24 = f32[1,128,2048]{2,1,0:T(8,128)} copy(f32[1,128,2048]{2,1,0:T(8,128)} %get-tuple-element.18) | data formatting | bytes 2097152
  96.6 0.0 copy-done
  96.6 0.5 copy.25
Async XLA Ops:
  89.7 6.9 %copy-start = (f32[1,128]{1,0:T(1,128)S(1)}, f32[1,128]{1,0:T(1,128)}, u32[]{:S(2)}) copy-start(f32[1,128]{1,0:T(1,128)} %get-tuple-element.11) | copy-start | bytes 1540
